TPU v7x, 32 devices: a whole 2x2x4 slice. The times are simulated.
32 devices in a mesh: krow: 16 (over z, x, core), kcol: 2 (over y).
Axes of the slice: x: 2, y: 2, z: 4, core: 2. Of those that a mesh axis runs over, the one named last changes fastest.
Arguments:
- green: bfloat16 [4, 2, 16, 4, 256, 256], P(None, None, 'krow', 'kcol'), may hold values from -6 to 6
- screened: float32 [16, 4, 65536], P(None, None, ('krow', 'kcol')), may hold values from 0.1 to 1
Outputs:
- sigma: bfloat16 [4, 2, 16, 4, 256, 256], P(None, None, 'krow', 'kcol')
- dressed: bfloat16 [4, 2, 16, 4, 256, 256], P(None, None, 'krow', 'kcol')
All inputs are finite; a program needn't handle non-finite values.
Results may differ from a plain program's by a relative error of at most 0.0053.
Values may be sent and summed in bfloat16 or wider, within the bound.
A program may use at most 64 MiB of HBM per device.

v0:
```python
import functools
import math

import jax
import jax.numpy as jnp
from jax import lax
from jax.experimental import pallas as pl
from jax.experimental.pallas import tpu as pltpu
from jax.sharding import PartitionSpec as P

SUBLANES = 8
LANES = 128


def turn(values, count, size, sign):
    real, imag = values
    count = count * sign % size
    if count * 8 % size == 0:
        eighth = count * 8 // size
        half = math.sqrt(0.5)
        if eighth == 0:
            return real, imag
        if eighth == 2:
            return -imag, real
        if eighth == 4:
            return -real, -imag
        if eighth == 6:
            return imag, -real
        if eighth == 1:
            return (real - imag) * half, (real + imag) * half
        if eighth == 3:
            return (real + imag) * -half, (real - imag) * half
        if eighth == 5:
            return (imag - real) * half, (real + imag) * -half
        return (real + imag) * half, (imag - real) * half
    angle = 2.0 * math.pi * count / size
    cosine, sine = math.cos(angle), math.sin(angle)
    return real * cosine - imag * sine, real * sine + imag * cosine


def transform(values, sign):
    size = len(values)
    if size == 1:
        return values
    if size % 2:
        out = []
        for target in range(size):
            terms = [turn(v, target * source, size, sign) for source, v in enumerate(values)]
            out.append((sum(t[0] for t in terms), sum(t[1] for t in terms)))
        return out
    even = transform(values[0::2], sign)
    odd = transform(values[1::2], sign)
    low, high = [], []
    for t in range(size // 2):
        real, imag = turn(odd[t], t, size, sign)
        low.append((even[t][0] + real, even[t][1] + imag))
        high.append((even[t][0] - real, even[t][1] - imag))
    return low + high


CORES = 2
SPLIT_X = 2


def corrected(g_real, g_imag, s_real, s_imag):
    def times(left, right):
        return jnp.dot(left, right, preferred_element_type=jnp.float32)

    kern_real = (times(g_real, s_real) - times(g_imag, s_imag)).astype(jnp.bfloat16)
    kern_imag = (times(g_real, s_imag) + times(g_imag, s_real)).astype(jnp.bfloat16)
    corr_real = times(kern_real, g_real) - times(kern_imag, g_imag)
    corr_imag = times(kern_real, g_imag) + times(kern_imag, g_real)
    share = 1.0 / g_real.shape[-1]
    return (
        (g_real.astype(jnp.float32) + corr_real * share).astype(jnp.bfloat16),
        (g_imag.astype(jnp.float32) + corr_imag * share).astype(jnp.bfloat16),
    )


def kernel(
    grid_dims, mesh_dims, rows,
    green_far, weights_far, green, sigma, dressed,
    weights, arrived, results, middle, pair_weights,
    load_sems, out_sems, in_sems, back_out_sems, back_in_sems, near_sems, all_in,
):
    one, two = grid_dims
    row_count, column_count = mesh_dims
    devices = row_count * column_count
    energies, _, local, orbitals, _ = green.shape
    local_one, local_two = one // row_count, two // column_count
    my_row, my_column = lax.axis_index("krow"), lax.axis_index("kcol")
    me = my_row * column_count + my_column

    plane_rows = SPLIT_X * CORES
    layers = row_count // plane_rows
    half = layers // 2
    plane = plane_rows * column_count
    pillars = SPLIT_X * column_count
    z = lax.div(my_row, plane_rows)
    x = lax.rem(lax.div(my_row, CORES), SPLIT_X)
    core = lax.rem(my_row, CORES)
    y = my_column
    pillar = x * column_count + y

    def at_place(z_, x_, core_, y_):
        return ((z_ * SPLIT_X + x_) * CORES + core_, y_)

    def flat_of(place):
        return place[0] * column_count + place[1]

    def signal(sem, place):
        pl.semaphore_signal(
            sem, inc=1, device_id=place, device_id_type=pl.DeviceIdType.MESH
        )

    def strip(owner):
        return pl.ds(pl.multiple_of(owner * rows, rows), rows)

    def load(e):
        return pltpu.make_async_copy(green_far.at[e], green.at[e], load_sems.at[e])

    load_weights = pltpu.make_async_copy(weights_far, weights, load_sems.at[energies])

    barrier = pltpu.get_barrier_semaphore()
    last_place = (z == layers - 1) & (x == SPLIT_X - 1) & (y == column_count - 1)

    @pl.when(last_place)
    def _():
        signal(barrier, at_place(z, x, 1 - core, y))

    def flag(condition):
        return jnp.where(condition, 1, 0)

    heard = CORES * (flag(x > 0) + flag(y > 0) + flag(z > 0)) + flag(last_place) * (CORES - 1)

    @pl.when(heard > 0)
    def _():
        pl.semaphore_wait(barrier, heard)

    for c in range(CORES):
        @pl.when(z < layers - 1)
        def _():
            signal(barrier, at_place(z + 1, x, c, y))

        @pl.when(z >= half)
        def _():
            signal(near_sems.at[z - half], at_place(half - 1, x, c, y))

        @pl.when(x < SPLIT_X - 1)
        def _():
            signal(barrier, at_place(z, x + 1, c, y))

        @pl.when(y < column_count - 1)
        def _():
            signal(barrier, at_place(z, x, c, y + 1))

    @pl.when(last_place)
    def _():
        @pl.loop(1, row_count // CORES * column_count)
        def _(step):
            chip = row_count // CORES * column_count - 1 - step
            signal(all_in, (lax.div(chip, column_count) * CORES + core, lax.rem(chip, column_count)))

    def send(e, place):
        peer = flat_of(place)
        pltpu.make_async_remote_copy(
            src_ref=green_far.at[e, :, :, strip(peer), :],
            dst_ref=arrived.at[e, me],
            send_sem=out_sems.at[e],
            recv_sem=in_sems.at[e],
            device_id=place,
            device_id_type=pl.DeviceIdType.MESH,
        ).start()

    def send_pillar(z_):
        @pl.loop(0, energies)
        def _(e):
            for c in range(CORES):
                send(e, at_place(z_, x, lax.rem(core + c, CORES), y))

    @pl.when(z == half)
    def _():
        @pl.loop(0, half)
        def _(step):
            send_pillar(half - 1 - step)

    for e in range(energies):
        load(e).start()
    load_weights.start()

    @pl.when(z == half - 1)
    def _():
        @pl.loop(0, layers - half)
        def _(step):
            pl.semaphore_wait(near_sems.at[step], CORES)
            send_pillar(half + step)

    @pl.when(jnp.logical_not(last_place))
    def _():
        pl.semaphore_wait(all_in, 1)

    middle_layer = (z == half) | (z == half - 1)

    def each_peer(first_round, body):
        @pl.loop(0, pillars)
        def _(turn_):
            to = lax.rem(pillar + 1 + turn_, pillars)
            own = turn_ == pillars - 1

            @pl.loop(0, layers)
            def _(step):
                z_ = lax.rem(z + step, layers)
                across = (z_ >= half) != (z >= half)
                done = flag(own & (step == 0))
                if first_round:
                    done = jnp.where(own & middle_layer & across, CORES, done)

                @pl.loop(done, CORES)
                def _(c):
                    body(at_place(
                        z_, lax.div(to, column_count), lax.rem(core + c, CORES),
                        lax.rem(to, column_count),
                    ))

    @pl.loop(0, energies)
    def _(e):
        each_peer(True, lambda place: send(e, place))

    def wait_all(part, sem):
        pltpu.make_async_copy(part, part, sem).wait()

    def others(buffer, e):
        return buffer.at[e, pl.ds(0, devices - 1)]

    def slot(k1, k2):
        return (
            (k1 // local_one) * column_count + k2 // local_two,
            (k1 % local_one) * local_two + k2 % local_two,
        )

    scale = -1.0 / (one * two)
    load_weights.wait()

    @pl.loop(0, one)
    def _(r1):
        for r2 in range(two):
            for row in range(rows):
                part = weights[r1, r2:r2 + 1, row * orbitals:(row + 1) * orbitals]
                pair_weights[r1, r2, row:row + 1, :] = part * scale

    def transform_energy(e):
        load(e).wait()
        wait_all(others(arrived, e), in_sems.at[e])
        arrived[e, me] = green[e, :, :, strip(me), :]

        @pl.loop(0, orbitals // LANES)
        def _(h):
            lanes = pl.ds(pl.multiple_of(h * LANES, LANES), LANES)
            for k2 in range(two):
                values = []
                for k1 in range(one):
                    s, at = slot(k1, k2)
                    values.append(tuple(
                        arrived[e, s, c, at, :, lanes].astype(jnp.float32) for c in range(2)
                    ))
                for r1, v in enumerate(transform(values, 1)):
                    middle[r1, k2, 0] = v[0]
                    middle[r1, k2, 1] = v[1]
            for r1 in range(one):
                values = transform([(middle[r1, k2, 0], middle[r1, k2, 1]) for k2 in range(two)], 1)
                for r2 in range(two):
                    weight = pair_weights[r1, r2, :, lanes]
                    values[r2] = (values[r2][0] * weight, values[r2][1] * weight)
                for k2, v in enumerate(transform(values, -1)):
                    middle[r1, k2, 0] = v[0]
                    middle[r1, k2, 1] = v[1]
            for k2 in range(two):
                values = [(middle[r1, k2, 0], middle[r1, k2, 1]) for r1 in range(one)]
                for k1, v in enumerate(transform(values, -1)):
                    s, at = slot(k1, k2)
                    for c in range(2):
                        results[e, s, c, at, :, lanes] = v[c].astype(jnp.bfloat16)

    def send_back(e):
        def one_send(place):
            pltpu.make_async_remote_copy(
                src_ref=results.at[e, flat_of(place)],
                dst_ref=sigma.at[e, :, :, strip(me), :],
                send_sem=back_out_sems.at[e],
                recv_sem=back_in_sems.at[e],
                device_id=place,
                device_id_type=pl.DeviceIdType.MESH,
            ).start()

        each_peer(False, one_send)

    last = energies - 1

    @pl.loop(0, energies)
    def _(e):
        transform_energy(e)

        send_back(e)
        sigma[e, :, :, strip(me), :] = results[e, me]

    @pl.loop(0, last)
    def _(e):
        wait_all(others(results, e), back_in_sems.at[e])

        @pl.loop(0, local)
        def _(at):
            real, imag = corrected(
                green[e, 0, at], green[e, 1, at], sigma[e, 0, at], sigma[e, 1, at]
            )
            dressed[e, 0, at] = real
            dressed[e, 1, at] = imag

    @pl.loop(0, last)
    def _(e):
        wait_all(others(arrived, e), out_sems.at[e])
        wait_all(others(results, e), back_out_sems.at[e])

    wait_all(others(arrived, last), out_sems.at[last])
    wait_all(others(results, last), back_out_sems.at[last])
    wait_all(others(results, last), back_in_sems.at[last])


def finish(green, sigma, dressed, sigma_far, dressed_far, piece, sems):
    energies, _, local, _, _ = green.shape
    last = energies - 1
    copies = [
        pltpu.make_async_copy(sigma, sigma_far, sems.at[local]),
        pltpu.make_async_copy(
            dressed.at[pl.ds(0, last)], dressed_far.at[pl.ds(0, last)], sems.at[local + 1]
        ),
    ]
    for copy in copies:
        copy.start()
    for at in range(local):
        piece[at, 0], piece[at, 1] = corrected(
            green[last, 0, at], green[last, 1, at], sigma[last, 0, at], sigma[last, 1, at]
        )
        copies.append(
            pltpu.make_async_copy(piece.at[at], dressed_far.at[last, :, at], sems.at[at])
        )
        copies[-1].start()
    for copy in copies:
        copy.wait()


def exchange_in_kernel(green, screened):
    mesh_dims = (lax.axis_size("krow"), lax.axis_size("kcol"))
    devices = mesh_dims[0] * mesh_dims[1]
    energies, _, local_one, local_two, orbitals, _ = green.shape
    grid_dims = screened.shape[:2]
    rows = orbitals // devices
    local = local_one * local_two
    layers = mesh_dims[0] // (SPLIT_X * CORES)
    flat = (energies, 2, local, orbitals, orbitals)
    block = (energies, devices, 2, local, rows, orbitals)
    vmem = pl.BlockSpec(memory_space=pltpu.VMEM)
    far = pl.BlockSpec(memory_space=pltpu.HBM)
    held = pl.pallas_call(
        functools.partial(kernel, grid_dims, mesh_dims, rows),
        out_shape=[pltpu.VMEM(flat, jnp.bfloat16)] * 3,
        in_specs=[far, far],
        out_specs=[vmem] * 3,
        scratch_shapes=[
            pltpu.VMEM(screened.shape, jnp.float32),
            pltpu.VMEM(block, jnp.bfloat16),
            pltpu.VMEM(block, jnp.bfloat16),
            pltpu.VMEM(grid_dims + (2, rows, LANES), jnp.float32),
            pltpu.VMEM(grid_dims + (rows, orbitals), jnp.float32),
            pltpu.SemaphoreType.DMA((energies + 1,)),
            pltpu.SemaphoreType.DMA((energies,)),
            pltpu.SemaphoreType.DMA((energies,)),
            pltpu.SemaphoreType.DMA((energies,)),
            pltpu.SemaphoreType.DMA((energies,)),
            pltpu.SemaphoreType.REGULAR((layers - layers // 2,)),
            pltpu.SemaphoreType.REGULAR,
        ],
        compiler_params=pltpu.CompilerParams(
            collective_id=0, has_side_effects=True, vmem_limit_bytes=15 * math.prod(block)
        ),
    )(*(
        pltpu.with_memory_space_constraint(v, pltpu.HBM) for v in (green.reshape(flat), screened)
    ))
    sigma, dressed = pl.pallas_call(
        finish,
        out_shape=[jax.ShapeDtypeStruct(flat, jnp.bfloat16)] * 2,
        in_specs=[vmem] * 3,
        out_specs=[far] * 2,
        scratch_shapes=[
            pltpu.VMEM((local, 2, orbitals, orbitals), jnp.bfloat16),
            pltpu.SemaphoreType.DMA((local + 2,)),
        ],
        compiler_params=pltpu.CompilerParams(vmem_limit_bytes=8 * math.prod(block)),
    )(*held)
    return sigma.reshape(green.shape), dressed.reshape(green.shape)


full_turn = 2.0 * math.pi


def phase_tables(length, forward):
    step_counter = jnp.arange(length, dtype=jnp.int32)
    product = step_counter[:, None] * step_counter[None, :] % length
    angles = full_turn * product.astype(jnp.float32) / length
    if forward:
        return (jnp.cos(angles) / length, jnp.sin(angles) / length)
    return (jnp.cos(angles), -jnp.sin(angles))


def apply_over_axis(matrix, values, along_dim):
    letters = "abcdefgh"[: values.ndim]
    target = letters[:along_dim] + "z" + letters[along_dim + 1 :]
    formula = "z" + letters[along_dim] + "," + letters + "->" + target
    return jnp.einsum(formula, matrix, values, precision=lax.Precision.HIGHEST)


def complex_along(state, cosine, sine, along_dim):
    real_part, imag_part = state
    out_real = apply_over_axis(cosine, real_part, along_dim) - apply_over_axis(
        sine, imag_part, along_dim
    )
    out_imag = apply_over_axis(sine, real_part, along_dim) + apply_over_axis(
        cosine, imag_part, along_dim
    )
    return (out_real, out_imag)


def weigh_back(state, weights, lead_one, lead_two):
    state = (-weights * state[0], -weights * state[1])
    cos_one, sin_one = phase_tables(lead_one, False)
    state = complex_along(state, cos_one, sin_one, 1)
    cos_two, sin_two = phase_tables(lead_two, False)
    state = complex_along(state, cos_two, sin_two, 2)
    return jnp.stack(state, 1).astype(jnp.bfloat16)


def whole_local(pieces, weights):
    state = (pieces[:, 0].astype(jnp.float32), pieces[:, 1].astype(jnp.float32))
    cos_two, sin_two = phase_tables(pieces.shape[3], True)
    state = complex_along(state, cos_two, sin_two, 2)
    cos_one, sin_one = phase_tables(pieces.shape[2], True)
    state = complex_along(state, cos_one, sin_one, 1)
    return weigh_back(state, weights, pieces.shape[2], pieces.shape[3])


def matmul_batch(left, right):
    return jnp.einsum("eklij,ekljm->eklim", left, right, preferred_element_type=jnp.float32)


def per_device(green, screened):
    krow_count = lax.axis_size("krow")
    momentum_column_count = lax.axis_size("kcol")
    orbitals = green.shape[4]
    slice_len = orbitals * green.shape[5] // (krow_count * momentum_column_count)
    blocks = green.reshape(green.shape[:4] + (krow_count, momentum_column_count, slice_len))
    weights = screened.reshape(screened.shape[0], screened.shape[1], 1, 1, screened.shape[2])
    gathered = lax.all_to_all(
        lax.all_to_all(blocks, "krow", split_axis=4, concat_axis=2, tiled=True),
        "kcol",
        split_axis=5,
        concat_axis=3,
        tiled=True,
    )
    middle = whole_local(gathered, weights)
    partway = lax.all_to_all(middle, "krow", split_axis=2, concat_axis=4, tiled=True)
    returned = lax.all_to_all(partway, "kcol", split_axis=3, concat_axis=5, tiled=True)
    sigma = returned.reshape(green.shape)
    green_real = green[:, 0]
    green_imag = green[:, 1]
    self_energy_real = sigma[:, 0]
    self_energy_imaginary = sigma[:, 1]
    kern_real = (
        matmul_batch(green_real, self_energy_real) - matmul_batch(green_imag, self_energy_imaginary)
    ).astype(jnp.bfloat16)
    kern_imag = (
        matmul_batch(green_real, self_energy_imaginary) + matmul_batch(green_imag, self_energy_real)
    ).astype(jnp.bfloat16)
    corr_real = matmul_batch(kern_real, green_real) - matmul_batch(kern_imag, green_imag)
    corr_imag = matmul_batch(kern_real, green_imag) + matmul_batch(kern_imag, green_real)
    dressed_real = green_real.astype(jnp.float32) + corr_real / orbitals
    dressed_imag = green_imag.astype(jnp.float32) + corr_imag / orbitals
    dressed = jnp.stack((dressed_real, dressed_imag), 1).astype(jnp.bfloat16)
    return (sigma, dressed)


def choose(green, screened):
    devices = lax.axis_size("krow") * lax.axis_size("kcol")
    orbitals = green.shape[4]
    shaped = lax.axis_size("krow") % (2 * SPLIT_X * CORES) == 0 and lax.axis_size("kcol") > 1
    if shaped and orbitals % (devices * SUBLANES) == 0 and orbitals % LANES == 0:
        return exchange_in_kernel(green, screened)
    return per_device(green, screened)


def solution(mesh):
    placed = (P(None, None, "krow", "kcol", None, None), P(None, None, ("krow", "kcol")))
    return jax.shard_map(
        choose,
        mesh=mesh,
        in_specs=placed,
        out_specs=(
            P(None, None, "krow", "kcol", None, None),
            P(None, None, "krow", "kcol", None, None),
        ),
        check_vma=False,
    )
```

profile of v0, /device:TPU:15, one launch (start us, length us, event | category | flops | bytes accessed | tf_op | source)
XLA Modules:
  0.0 97.2 jit_solution(3034699152202194559)
XLA Ops:
  0.6 94.5 %shard_map.41 = (bf16[4,2,2,256,256]{4,3,2,1,0:T(8,128)(2,1)S(1)}, bf16[4,2,2,256,256]{4,3,2,1,0:T(8,128)(2,1)S(1)}, bf16[4,2,2,256,256]{4,3,2,1,0:T(8,128)(2,1)S(1)}) custom-call(bf16[4,2,2,256,256]{4,3,2,1,0:T(8,128)(2,1)} %bitcast.7, f32[16,4,2048]{2,1,0:T(4,128)} %weights_far.1), custom_call_target="tpu_custom_call" | custom-call | tf_op jit(solution)/shard_map/pallas_call | solution.py:363
  95.2 2.0 %shard_map.42 = (bf16[4,2,2,256,256]{4,3,2,1,0:T(8,128)(2,1)}, bf16[4,2,2,256,256]{4,3,2,1,0:T(8,128)(2,1)}) custom-call(bf16[4,2,2,256,256]{4,3,2,1,0:T(8,128)(2,1)S(1)} %get-tuple-element.7.green, bf16[4,2,2,256,256]{4,3,2,1,0:T(8,128)(2,1)S(1)} %get-tuple-element.8.sigma, bf16[4,2,2,256,256]{4,3,2,1,0:T(8,128)(2,1)S(1)} %get-tuple-element.9.dressed), custom_call_target="tpu_custom_call" | custom-call | tf_op jit(solution)/shard_map/pallas_call | solution.py:388
where the time goes:
time: 98.3 us; the launch traced here: 97.2 us
  Pallas kernels  96.6 us (98%)
    pallas_call x1, Pallas kernels, exchange_in_kernel(): pl.pallas_call(functools.partial(kernel, grid_dims, mesh_dims, rows), out...  94.5 us
    pallas_call x1, Pallas kernels, exchange_in_kernel(): pl.pallas_call(finish, out_shape=[jax.ShapeDtypeStruct(flat, jnp.bfloat16...  2.03 us

commit v1 on v0

--- a/solution.py
+++ b/solution.py
@@ -60,6 +60,7 @@
 
 CORES = 2
 SPLIT_X = 2
+PILLAR_ORDER = ((1, 0, 2, 3), (2, 0, 3, 1), (0, 1, 3, 2), (0, 2, 1, 3))
 
 
 def corrected(g_real, g_imag, s_real, s_imag):
@@ -201,11 +202,20 @@
 
     middle_layer = (z == half) | (z == half - 1)
 
+    def next_pillar(turn_):
+        if pillars != len(PILLAR_ORDER):
+            return lax.rem(pillar + 1 + turn_, pillars)
+        to = 0
+        for source, order in enumerate(PILLAR_ORDER):
+            for when, target_ in enumerate(order):
+                to = to + jnp.where((pillar == source) & (turn_ == when), target_, 0)
+        return to
+
     def each_peer(first_round, body):
         @pl.loop(0, pillars)
         def _(turn_):
-            to = lax.rem(pillar + 1 + turn_, pillars)
-            own = turn_ == pillars - 1
+            to = next_pillar(turn_)
+            own = to == pillar
 
             @pl.loop(0, layers)
             def _(step):

time: 98.3 us -> 98.1 us (level)
  no operation moved by 1% of the time
where the time goes in v1:
time: 98.1 us; the launch traced here: 97.3 us
  Pallas kernels  96.6 us (98%)
    pallas_call x1, Pallas kernels, exchange_in_kernel(): pl.pallas_call(functools.partial(kernel, grid_dims, mesh_dims, rows), out...  94.6 us
    pallas_call x1, Pallas kernels, exchange_in_kernel(): pl.pallas_call(finish, out_shape=[jax.ShapeDtypeStruct(flat, jnp.bfloat16...  2.03 us

profile of v1, /device:TPU:15, one launch (start us, length us, event | category | flops | bytes accessed | tf_op | source)
XLA Modules:
  0.0 97.3 jit_solution(2199776132466899205)
XLA Ops:
  0.6 94.6 %shard_map.41 = (bf16[4,2,2,256,256]{4,3,2,1,0:T(8,128)(2,1)S(1)}, bf16[4,2,2,256,256]{4,3,2,1,0:T(8,128)(2,1)S(1)}, bf16[4,2,2,256,256]{4,3,2,1,0:T(8,128)(2,1)S(1)}) custom-call(bf16[4,2,2,256,256]{4,3,2,1,0:T(8,128)(2,1)} %bitcast.7, f32[16,4,2048]{2,1,0:T(4,128)} %weights_far.1), custom_call_target="tpu_custom_call" | custom-call | tf_op jit(solution)/shard_map/pallas_call | solution.py:373
  95.2 2.0 %shard_map.42 = (bf16[4,2,2,256,256]{4,3,2,1,0:T(8,128)(2,1)}, bf16[4,2,2,256,256]{4,3,2,1,0:T(8,128)(2,1)}) custom-call(bf16[4,2,2,256,256]{4,3,2,1,0:T(8,128)(2,1)S(1)} %get-tuple-element.7.green, bf16[4,2,2,256,256]{4,3,2,1,0:T(8,128)(2,1)S(1)} %get-tuple-element.8.sigma, bf16[4,2,2,256,256]{4,3,2,1,0:T(8,128)(2,1)S(1)} %get-tuple-element.9.dressed), custom_call_target="tpu_custom_call" | custom-call | tf_op jit(solution)/shard_map/pallas_call | solution.py:398

commit v2 on v1

--- a/solution.py
+++ b/solution.py
@@ -212,25 +212,25 @@
         return to
 
     def each_peer(first_round, body):
-        @pl.loop(0, pillars)
-        def _(turn_):
+        @pl.loop(0, pillars * layers)
+        def _(n):
+            paired = (z >= half) & (pillar > 0)
+            step = jnp.where(paired, lax.rem(lax.div(n, 2), layers), lax.rem(n, layers))
+            turn_ = jnp.where(paired, lax.div(n, 2 * layers) * 2 + lax.rem(n, 2), lax.div(n, layers))
             to = next_pillar(turn_)
             own = to == pillar
-
-            @pl.loop(0, layers)
-            def _(step):
-                z_ = lax.rem(z + step, layers)
-                across = (z_ >= half) != (z >= half)
-                done = flag(own & (step == 0))
-                if first_round:
-                    done = jnp.where(own & middle_layer & across, CORES, done)
-
-                @pl.loop(done, CORES)
-                def _(c):
-                    body(at_place(
-                        z_, lax.div(to, column_count), lax.rem(core + c, CORES),
-                        lax.rem(to, column_count),
-                    ))
+            z_ = lax.rem(z + step, layers)
+            across = (z_ >= half) != (z >= half)
+            done = flag(own & (step == 0))
+            if first_round:
+                done = jnp.where(own & middle_layer & across, CORES, done)
+
+            @pl.loop(done, CORES)
+            def _(c):
+                body(at_place(
+                    z_, lax.div(to, column_count), lax.rem(core + c, CORES),
+                    lax.rem(to, column_count),
+                ))
 
     @pl.loop(0, energies)
     def _(e):

time: 98.1 us -> 97.9 us (level)
  no operation moved by 1% of the time
where the time goes in v2:
time: 97.9 us; the launch traced here: 97.2 us
  Pallas kernels  96.6 us (99%)
    pallas_call x1, Pallas kernels, exchange_in_kernel(): pl.pallas_call(functools.partial(kernel, grid_dims, mesh_dims, rows), out...  94.5 us
    pallas_call x1, Pallas kernels, exchange_in_kernel(): pl.pallas_call(finish, out_shape=[jax.ShapeDtypeStruct(flat, jnp.bfloat16...  2.03 us

profile of v2, /device:TPU:15, one launch (start us, length us, event | category | flops | bytes accessed | tf_op | source)
XLA Modules:
  0.0 97.2 jit_solution(14079655381624527767)
XLA Ops:
  0.6 94.5 %shard_map.41 = (bf16[4,2,2,256,256]{4,3,2,1,0:T(8,128)(2,1)S(1)}, bf16[4,2,2,256,256]{4,3,2,1,0:T(8,128)(2,1)S(1)}, bf16[4,2,2,256,256]{4,3,2,1,0:T(8,128)(2,1)S(1)}) custom-call(bf16[4,2,2,256,256]{4,3,2,1,0:T(8,128)(2,1)} %bitcast.7, f32[16,4,2048]{2,1,0:T(4,128)} %weights_far.1), custom_call_target="tpu_custom_call" | custom-call | tf_op jit(solution)/shard_map/pallas_call | solution.py:373
  95.2 2.0 %shard_map.42 = (bf16[4,2,2,256,256]{4,3,2,1,0:T(8,128)(2,1)}, bf16[4,2,2,256,256]{4,3,2,1,0:T(8,128)(2,1)}) custom-call(bf16[4,2,2,256,256]{4,3,2,1,0:T(8,128)(2,1)S(1)} %get-tuple-element.7.green, bf16[4,2,2,256,256]{4,3,2,1,0:T(8,128)(2,1)S(1)} %get-tuple-element.8.sigma, bf16[4,2,2,256,256]{4,3,2,1,0:T(8,128)(2,1)S(1)} %get-tuple-element.9.dressed), custom_call_target="tpu_custom_call" | custom-call | tf_op jit(solution)/shard_map/pallas_call | solution.py:398
